TPU v7x, 32 devices: a whole 2x2x4 slice. The times are simulated.
32 devices in a mesh: dp: 4 (over z), expert: 4 (over y, core), tensor: 2 (over x).
Axes of the slice: x: 2, y: 2, z: 4, core: 2. Of those that a mesh axis runs over, the one named last changes fastest.
Arguments:
- hidden: bfloat16 [2048, 6144], P(('dp', 'expert'), 'tensor'), may hold values from -6 to 6
- expert_ids: int32 [2048, 8], P(('dp', 'expert')), may hold values from 0 to 383, as said below
- gate_fixed: int32 [2048, 8], P(('dp', 'expert')), may hold values from 4096 to 65535
- slot_expert: int32 [16], replicated, may hold values from 0 to 383, as said below
- expert_in: bfloat16 [16, 6144, 2, 1024], P(('dp', 'expert'), 'tensor'), may hold values from -1 to 1, as said below
- expert_out: bfloat16 [16, 1024, 6144], P(('dp', 'expert'), None, 'tensor'), may hold values from -1 to 1, as said below
- shared_in: bfloat16 [6144, 2, 1024], P('tensor', None, 'dp'), may hold values from -0.078125 to 0.078125
- shared_out: bfloat16 [1024, 6144], P('dp', 'tensor'), may hold values from -0.1875 to 0.1875
Outputs:
- mixed: bfloat16 [2048, 6144], P(('dp', 'expert'), 'tensor')
Inputs may be any that keep to these rules, and one draw needn't show every extreme that they name: `expert_ids`: each row names 8 different experts. `slot_expert`: 14 different experts fill the 16 slots; 2 of them hold two slots each, the others one. `expert_in`: slots that hold the same expert hold the same weights. `expert_out`: slots that hold the same expert hold the same weights.
All inputs are finite; a program needn't handle non-finite values.
Results may differ from a plain program's by a relative error of at most 0.006.
Values may be sent and summed in bfloat16 or wider, within the bound.
A program may use at most 192 MiB of HBM per device.

v0:
```python
import jax
import jax.numpy as jnp
from jax import lax
from jax.sharding import PartitionSpec as P

EXPERTS = 384
CAP = 4
gate_scale = 1.0 / 65536.0


def swiglu(pre):
    return (jax.nn.silu(pre[:, 0, :]) * pre[:, 1, :]).astype(jnp.bfloat16)


def route_plan(chosen, row_rank, slot_expert):
    slot_count = slot_expert.shape[0]
    slot_iota = jnp.arange(slot_count, dtype=jnp.int32)[:, None]
    owns = slot_expert[:, None] == jnp.arange(chosen.shape[2], dtype=jnp.int32)[None, :]
    home = jnp.min(jnp.where(owns, slot_iota, slot_count), axis=0)
    spare = jnp.min(jnp.where(owns & (slot_iota != home[None, :]), slot_iota, slot_count), axis=0)
    home_of = jnp.sum(jnp.where(chosen, home[None, None, :], 0), axis=2)
    spare_of = jnp.sum(jnp.where(chosen, spare[None, None, :], 0), axis=2)
    first = row_rank < CAP
    spill = (row_rank >= CAP) & (row_rank < 2 * CAP) & (spare_of < slot_count)
    target = jnp.where(first, home_of, jnp.where(spill, spare_of, slot_count))
    slot_row = jnp.where(first, row_rank, row_rank - CAP)
    return (target, slot_row)


def dispatch_rows(send_rows):
    return lax.all_to_all(send_rows, ("dp", "expert"), split_axis=0, concat_axis=0, tiled=True)


def return_rows(answers):
    return lax.all_to_all(answers, ("dp", "expert"), split_axis=0, concat_axis=0, tiled=True)


def shards(
    hidden, expert_ids, gate_fixed, slot_expert, expert_in, expert_out, shared_in, shared_out
):
    tok_rows, half_width = hidden.shape
    topk_count = expert_ids.shape[1]
    slot_count = slot_expert.shape[0]
    experts_iota = jnp.arange(EXPERTS, dtype=jnp.int32)
    chosen = expert_ids[:, :, None] == experts_iota[None, None, :]
    picked = jnp.any(chosen, axis=1).astype(jnp.bfloat16)
    token_iota = jnp.arange(tok_rows, dtype=jnp.int32)
    earlier = (token_iota[:, None] > token_iota[None, :]).astype(jnp.bfloat16)
    before = jnp.dot(earlier, picked, preferred_element_type=jnp.float32)
    row_rank = jnp.sum(jnp.where(chosen, before[:, None, :], 0.0), axis=2).astype(jnp.int32)
    target, slot_row = route_plan(chosen, row_rank, slot_expert)
    flat_row = jnp.where(target < slot_count, target * CAP + slot_row, -1)
    row_iota = jnp.arange(slot_count * CAP, dtype=jnp.int32)
    owner = jnp.repeat(token_iota, topk_count)
    match_rows = flat_row.reshape(-1)[:, None] == row_iota[None, :]
    source_token = jnp.max(jnp.where(match_rows, owner[:, None], -1), axis=0)
    fetched_rows = jnp.take(hidden, jnp.maximum(source_token, 0), axis=0)
    send_rows = jnp.where(source_token[:, None] >= 0, fetched_rows, jnp.zeros((), jnp.bfloat16))
    piece = lax.all_gather(hidden, "dp", axis=0, tiled=True)
    partial_value = jnp.dot(
        piece, shared_in.reshape(half_width, -1), preferred_element_type=jnp.float32
    )
    shared_partial = partial_value.reshape(piece.shape[0], 2, -1)
    arrived = dispatch_rows(send_rows.reshape(slot_count, CAP, half_width))
    rows = arrived.reshape(-1, half_width)
    partial_value = jnp.dot(
        rows, expert_in[0].reshape(half_width, -1), preferred_element_type=jnp.float32
    )
    routed_partial = partial_value.reshape(rows.shape[0], 2, -1)
    shared_half, routed_half = (
        lax.psum_scatter(shared_partial, "tensor", scatter_dimension=2, tiled=True),
        lax.psum_scatter(routed_partial, "tensor", scatter_dimension=2, tiled=True),
    )
    shared_act, routed_act = (
        lax.all_gather(swiglu(shared_half), "tensor", axis=1, tiled=True),
        lax.all_gather(swiglu(routed_half), "tensor", axis=1, tiled=True),
    )
    shared_part = lax.psum_scatter(
        jnp.dot(shared_act, shared_out, preferred_element_type=jnp.float32),
        "dp",
        scatter_dimension=0,
        tiled=True,
    )
    answers = jnp.dot(routed_act, expert_out[0], preferred_element_type=jnp.float32).astype(
        jnp.bfloat16
    )
    returned = return_rows(answers.reshape(slot_count, CAP, half_width))
    returned = returned.reshape(-1, half_width)
    gates = gate_fixed.astype(jnp.float32) * gate_scale
    routed = jnp.zeros((tok_rows, half_width), jnp.float32)
    for column in range(topk_count):
        index = flat_row[:, column]
        answer_rows = jnp.take(returned, jnp.maximum(index, 0), axis=0).astype(jnp.float32)
        routed = routed + jnp.where(
            index[:, None] >= 0, gates[:, column : column + 1] * answer_rows, 0.0
        )
    return (shared_part + routed).astype(jnp.bfloat16)


def solution(mesh):
    in_specs = (
        P(("dp", "expert"), "tensor"),
        P(("dp", "expert"), None),
        P(("dp", "expert"), None),
        P(),
        P(("dp", "expert"), "tensor", None, None),
        P(("dp", "expert"), None, "tensor"),
        P("tensor", None, "dp"),
        P("dp", "tensor"),
    )
    out_specs = P(("dp", "expert"), "tensor")
    return jax.shard_map(shards, mesh=mesh, in_specs=in_specs, out_specs=out_specs, check_vma=False)
```

profile of v0, /device:TPU:8, one launch (start us, length us, event | category | flops | bytes accessed | tf_op | source)
XLA Modules:
  0.0 273.9 jit_solution(13360742678209995366)
XLA Ops:
  7.3 0.8 copy.22
  9.6 4.8 %select_reduce_fusion = (s32[128,8]{1,0:T(8,128)S(1)}, s32[128,8]{1,0:T(8,128)S(1)}) fusion(s32[384]{0:T(512)S(1)} %select_reduce_fusion.4, s32[128,8]{1,0:T(8,128)S(1)} %copy.22, s32[384]{0:T(512)S(1)} %select_reduce_fusion.5), kind=kLoop, calls=%fused_computation.15 | loop fusion | flops 1964032 | bytes 15360 | tf_op jit(solution)/shard_map/reduce_sum | solution.py:22
  16.3 0.8 gather_fusion
  17.2 4.4 %copy.24 = bf16[384,8,2,256]{3,1,2,0:T(8,128)(2,1)} copy(bf16[384,8,2,256]{3,2,1,0:T(2,128)(2,1)} %bitcast.66) | data formatting | bytes 6291456
  21.6 4.7 %copy.21 = bf16[512,3072]{1,0:T(8,128)(2,1)} copy(bf16[512,3072]{0,1:T(8,128)(2,1)} %bitcast.65) | data formatting | bytes 6291456 | tf_op jit(solution)/shard_map/dot_general | solution.py:60
  26.3 45.1 %all-gather.2.cloned.1.call-done = bf16[512,3072]{1,0:T(8,128)(2,1)} async-done(((bf16[128,3072]{1,0:T(8,128)(2,1)}), bf16[512,3072]{1,0:T(8,128)(2,1)}) %all-gather.2.cloned.1.call-update) | async-done | bytes 3145744 | tf_op jit(solution)/shard_map/all_gather | solution.py:59
  71.4 5.7 %fusion.5 = f32[512,2,256]{2,0,1:T(8,128)} fusion(bf16[2,256,3072]{2,1,0:T(8,128)(2,1)} %bitcast.67, bf16[512,3072]{1,0:T(8,128)(2,1)} %all-gather.2.cloned.1.call-done), kind=kOutput, calls=%fused_computation.12 | convolution fusion | flops 1610612736 | bytes 7340032 | tf_op jit(solution)/shard_map/dot_general | solution.py:60
  77.1 1.1 select_select_fusion
  78.2 6.1 %all-to-all-start = ((bf16[16,4,3072]{2,1,0:T(4,128)(2,1)}), bf16[16,4,3072]{2,1,0:T(4,128)(2,1)S(1)}, u32[]{:S(2)}, u32[]{:S(2)}) async-start(bf16[16,4,3072]{2,1,0:T(4,128)(2,1)} %select_select_fusion), calls=%async_computation.2 | async-start | bytes 786432 | tf_op jit(solution)/shard_map/all_to_all | solution.py:31
  84.6 13.0 %copy.25 = bf16[384,8,2,1024]{3,1,2,0:T(8,128)(2,1)} copy(bf16[384,8,2,1024]{3,2,1,0:T(2,128)(2,1)} %bitcast.64) | data formatting | bytes 25165824
  97.6 16.7 %copy.23 = bf16[2048,3072]{1,0:T(8,128)(2,1)} copy(bf16[2048,3072]{0,1:T(8,128)(2,1)} %bitcast.63) | data formatting | bytes 25165824 | tf_op jit(solution)/shard_map/dot_general | solution.py:66
  114.3 9.3 %fusion.19 = f32[64,2,1024]{2,0,1:T(8,128)} fusion(bf16[64,3072,1]{1,0,2:T(8,128)(2,1)S(1)} %reshape.214, bf16[2,1024,3072]{2,1,0:T(8,128)(2,1)} %bitcast.62), kind=kOutput, calls=%fused_computation.100 | convolution fusion | flops 805306368 | bytes 13500416 | tf_op jit(solution)/shard_map/dot_general | solution.py:66
  123.7 1.1 fusion.9
  124.8 6.2 %all_gather.10 = bf16[512,256]{1,0:T(8,128)(2,1)S(1)} all-gather(bf16[512,128]{1,0:T(8,128)(2,1)S(1)} %fusion.9), channel_id=1, replica_groups=mesh['dp'=4,'expert'=4,'tensor'=2] {'tensor'}, dimensions={1}, use_global_device_ids=true | all-gather | bytes 393216 | tf_op jit(solution)/shard_map/all_gather | solution.py:75
  131.1 3.7 %fusion.18 = f32[512,3072]{1,0:T(8,128)} fusion(bf16[512,256]{1,0:T(8,128)(2,1)S(1)} %all_gather.10, bf16[256,3072]{1,0:T(8,128)(2,1)S(1)} %copy-done), kind=kOutput, calls=%fused_computation.99 | convolution fusion | flops 805306368 | bytes 8126464 | tf_op jit(solution)/shard_map/dot_general | solution.py:79
  135.8 3.6 %reduce-scatter.8.cloned.1.call-done = f32[64,2,512]{2,0,1:T(8,128)} async-done(((f32[64,2,1024]{2,0,1:T(8,128)}), f32[64,2,512]{2,0,1:T(8,128)}) %reduce-scatter.8.cloned.1.call-update) | async-done | bytes 262160 | tf_op jit(solution)/shard_map/reduce_scatter | solution.py:72
  139.3 1.0 fusion.11
  140.4 4.9 %all_gather.11 = bf16[64,1024]{1,0:T(8,128)(2,1)S(1)} all-gather(bf16[64,512]{1,0:T(8,128)(2,1)S(1)} %fusion.11), channel_id=1, replica_groups=mesh['dp'=4,'expert'=4,'tensor'=2] {'tensor'}, dimensions={1}, use_global_device_ids=true | all-gather | bytes 196608 | tf_op jit(solution)/shard_map/all_gather | solution.py:76
  145.3 4.2 %fusion.2 = bf16[64,3072]{1,0:T(8,128)(2,1)S(1)} fusion(bf16[64,1024]{1,0:T(8,128)(2,1)S(1)} %all_gather.11, bf16[1,1024,3072]{2,1,0:T(8,128)(2,1)} %param.15), kind=kOutput, calls=%fused_computation.11 | convolution fusion | flops 402849792 | bytes 6815744 | tf_op jit(solution)/shard_map/dot_general | solution.py:84
  149.6 0.9 reshape.114
  150.5 6.1 %all-to-all-start.1 = ((bf16[16,4,3072]{2,1,0:T(4,128)(2,1)}), bf16[16,4,3072]{2,1,0:T(4,128)(2,1)S(1)}, u32[]{:S(2)}, u32[]{:S(2)}) async-start(bf16[16,4,3072]{2,1,0:T(4,128)(2,1)} %reshape.114), calls=%async_computation.4 | async-start | bytes 786432 | tf_op jit(solution)/shard_map/all_to_all | solution.py:35
  156.6 23.3 %all-to-all-done.1 = bf16[16,4,3072]{2,1,0:T(4,128)(2,1)S(1)} async-done(((bf16[16,4,3072]{2,1,0:T(4,128)(2,1)}), bf16[16,4,3072]{2,1,0:T(4,128)(2,1)S(1)}, u32[]{:S(2)}, u32[]{:S(2)}) %all-to-all-start.1) | async-done | bytes 393248 | tf_op jit(solution)/shard_map/all_to_all | solution.py:35
  180.0 1.0 gather_fusion.2
  181.0 1.0 gather_fusion.3
  182.1 2.0 gather_fusion.4
  184.0 1.9 gather_fusion.5
  186.0 2.0 gather_fusion.6
  188.0 2.0 gather_fusion.7
  189.9 1.9 gather_fusion.8
  191.8 1.9 gather_fusion.1
  193.8 67.0 %reduce-scatter.6.cloned.1.call-done = f32[128,3072]{1,0:T(8,128)} async-done(((f32[512,3072]{1,0:T(8,128)}), f32[128,3072]{1,0:T(8,128)}) %reduce-scatter.6.cloned.1.call-update) | async-done | bytes 1572880 | tf_op jit(solution)/shard_map/reduce_scatter | solution.py:78
  260.8 6.6 %add_convert_fusion = bf16[128,3072]{1,0:T(8,128)(2,1)} fusion(f32[128,3072]{1,0:T(8,128)} %reduce-scatter.6.cloned.1.call-done, bf16[128,3072]{1,0:T(8,128)(2,1)} %gather_fusion.8, bf16[128,3072]{1,0:T(8,128)(2,1)} %gather_fusion.7, bf16[128,3072]{1,0:T(8,128)(2,1)} %gather_fusion.6, bf16[128,3072]{1,0:T(8,128)(2,1)} %gather_fusion.5, ...), kind=kLoop, calls=%fused_computation.14 | loop fusion | flops 16121856 | bytes 8656896 | tf_op jit(solution)/shard_map/convert_element_type | solution.py:97
  (60 shorter events, 5.6 us)
Async XLA Ops:
  6.5 124.5 %copy-start = (bf16[256,3072]{1,0:T(8,128)(2,1)S(1)}, bf16[256,3072]{1,0:T(8,128)(2,1)}, u32[]{:S(2)}) copy-start(bf16[256,3072]{1,0:T(8,128)(2,1)} %param.17) | copy-start | bytes 4718596
  6.5 9.7 %copy-start.2 = (bf16[128,3072]{1,0:T(8,128)(2,1)S(1)}, bf16[128,3072]{1,0:T(8,128)(2,1)}, u32[]{:S(2)}) copy-start(bf16[128,3072]{1,0:T(8,128)(2,1)} %param.10) | copy-start | bytes 2359300
  6.5 64.8 %all-gather.2.cloned.1.call-start = ((), (), s32[]{:S(2)}) async-start(), calls=%async_computation.5 | async-start | bytes 3932160 | tf_op jit(solution)/shard_map/all_gather | solution.py:59
  7.3 116.5 %reduce-scatter.4.cloned.1.call-start = ((), (), s32[]{:S(2)}) async-start(), calls=%async_computation.6 | async-start | bytes 1572864 | tf_op jit(solution)/shard_map/reduce_scatter | solution.py:71
  78.2 36.0 %all-to-all-start = ((bf16[16,4,3072]{2,1,0:T(4,128)(2,1)}), bf16[16,4,3072]{2,1,0:T(4,128)(2,1)S(1)}, u32[]{:S(2)}, u32[]{:S(2)}) async-start(bf16[16,4,3072]{2,1,0:T(4,128)(2,1)} %select_select_fusion), calls=%async_computation.2 | async-start | bytes 786432 | tf_op jit(solution)/shard_map/all_to_all | solution.py:31
  84.3 55.0 %reduce-scatter.8.cloned.1.call-start = ((), (), s32[]{:S(2)}) async-start(), calls=%async_computation.8 | async-start | bytes 786432 | tf_op jit(solution)/shard_map/reduce_scatter | solution.py:72
  123.6 137.1 %reduce-scatter.6.cloned.1.call-start = ((), (), s32[]{:S(2)}) async-start(), calls=%async_computation.7 | async-start | bytes 7864320 | tf_op jit(solution)/shard_map/reduce_scatter | solution.py:78
  149.5 7.0 %copy-start.3 = (s32[128,8]{0,1:T(8,128)S(1)}, s32[128,8]{0,1:T(8,128)}, u32[]{:S(2)}) copy-start(s32[128,8]{0,1:T(8,128)} %param.12) | copy-start | bytes 12292
  150.5 29.4 %all-to-all-start.1 = ((bf16[16,4,3072]{2,1,0:T(4,128)(2,1)}), bf16[16,4,3072]{2,1,0:T(4,128)(2,1)S(1)}, u32[]{:S(2)}, u32[]{:S(2)}) async-start(bf16[16,4,3072]{2,1,0:T(4,128)(2,1)} %reshape.114), calls=%async_computation.4 | async-start | bytes 786432 | tf_op jit(solution)/shard_map/all_to_all | solution.py:35
  260.8 6.6 %copy-start.1 = (bf16[256,3072]{1,0:T(8,128)(2,1)S(1)}, bf16[256,3072]{1,0:T(8,128)(2,1)}, u32[]{:S(2)}) copy-start(bf16[256,3072]{1,0:T(8,128)(2,1)} %param.17) | copy-start | bytes 4718596
Sparse Core Ops, SparseCore 0:
  8.9 62.4 all-gather.1
  77.2 21.2 reduce-scatter.3
  123.8 15.5 reduce-scatter.7
  141.5 119.2 reduce-scatter.5
where the time goes:
time: 275 us; the launch traced here: 274 us
  waiting for transfers between devices  140 us (51%)
  local copies, waits for them, and re-layouts  55.9 us (20%)
  matrix products  23.1 us (8%)
  other arithmetic  18 us (7%)
  between operations  13.4 us (5%)
  starting transfers between devices  12.5 us (5%)
  blocking collectives  11.2 us (4%)
    reduce_scatter x1, waiting for transfers between devices, shards(): lax.psum_scatter(jnp.dot(shared_act, shared_out, preferred_element_type=j...  67 us
    all_gather x1, waiting for transfers between devices, shards(): piece = lax.all_gather(hidden, 'dp', axis=0, tiled=True)  45.1 us
    all_to_all x1, waiting for transfers between devices, return_rows(): lax.all_to_all(answers, ('dp', 'expert'), split_axis=0, concat_axis=0, ti...  23.3 us
    unnamed x11, local copies, waits for them, and re-layouts  18.2 us
    dot_general x1, local copies, waits for them, and re-layouts, shards(): jnp.dot(rows, expert_in[0].reshape(half_width, -1), preferred_element_typ...  16.7 us
    gather x8, local copies, waits for them, and re-layouts, shards(): jnp.take(returned, jnp.maximum(index, 0), axis=0).astype(jnp.float32)  13.8 us
    dot_general x1, matrix products, shards(): jnp.dot(rows, expert_in[0].reshape(half_width, -1), preferred_element_typ...  9.29 us
    convert_element_type x1, other arithmetic, shards(): return (shared_part + routed).astype(jnp.bfloat16)  6.55 us
  transfers between devices with their start and end apart: 6, of which 4 were waited for; matrix products, arithmetic and copies ran while one was open for 31% of the time, Pallas kernels for 0%

commit v1 on v0

--- a/solution.py
+++ b/solution.py
@@ -56,7 +56,12 @@
     source_token = jnp.max(jnp.where(match_rows, owner[:, None], -1), axis=0)
     fetched_rows = jnp.take(hidden, jnp.maximum(source_token, 0), axis=0)
     send_rows = jnp.where(source_token[:, None] >= 0, fetched_rows, jnp.zeros((), jnp.bfloat16))
-    piece = lax.all_gather(hidden, "dp", axis=0, tiled=True)
+    ring = [hidden]
+    for hop in range(3):
+        ring.append(lax.ppermute(ring[-1], "dp", [(dev, (dev + 1) % 4) for dev in range(4)]))
+    piece = jnp.roll(
+        jnp.concatenate(ring[::-1], axis=0), (lax.axis_index("dp") + 1) * ring[0].shape[0], axis=0
+    )
     partial_value = jnp.dot(
         piece, shared_in.reshape(half_width, -1), preferred_element_type=jnp.float32
     )

time: 275 us -> 274 us (level)
  waiting for transfers between devices: 140 us -> 127 us
  local copies, waits for them, and re-layouts: 55.9 us -> 65.5 us
  starting transfers between devices: 12.5 us -> 17.1 us
  matrix products: 23.1 us -> 20.1 us
    all_gather x1 -> x0, waiting for transfers between devices: 45.1 us -> none  [shards(): piece = lax.all_gather(hidden, 'dp', axis=0, tiled=True)]
    ppermute x0 -> x3, waiting for transfers between devices: none -> 34 us  [shards(): lax.ppermute(ring[-1], 'dp', [(dev, (dev + 1) % 4) for dev in range(4)])]
    unnamed x11 -> x32, local copies, waits for them, and re-layouts: 18.2 us -> 26.1 us
    ppermute x0 -> x3, starting transfers between devices: none -> 3.85 us  [shards(): lax.ppermute(ring[-1], 'dp', [(dev, (dev + 1) % 4) for dev in range(4)])]
    dot_general x1, matrix products: 5.73 us -> 2.89 us  [shards(): jnp.dot(piece, shared_in.reshape(half_width, -1), preferred_element_type=...]
  transfers between devices with their start and end apart: 6 -> 8, of which waited for: 4 -> 6; matrix products, arithmetic and copies ran while one was open for 31% -> 32% of each run, Pallas kernels for 0% -> 0%
where the time goes in v1:
time: 274 us; the launch traced here: 272 us
  waiting for transfers between devices  127 us (46%)
  local copies, waits for them, and re-layouts  65.5 us (24%)
  matrix products  20.1 us (7%)
  other arithmetic  18.1 us (7%)
  starting transfers between devices  17.1 us (6%)
  between operations  13.5 us (5%)
  blocking collectives  11.2 us (4%)
    reduce_scatter x1, waiting for transfers between devices, shards(): lax.psum_scatter(jnp.dot(shared_act, shared_out, preferred_element_type=j...  67.2 us
    ppermute x3, waiting for transfers between devices, shards(): lax.ppermute(ring[-1], 'dp', [(dev, (dev + 1) % 4) for dev in range(4)])  34 us
    unnamed x32, local copies, waits for them, and re-layouts  26.1 us
    all_to_all x1, waiting for transfers between devices, return_rows(): lax.all_to_all(answers, ('dp', 'expert'), split_axis=0, concat_axis=0, ti...  23.4 us
    dot_general x1, local copies, waits for them, and re-layouts, shards(): jnp.dot(rows, expert_in[0].reshape(half_width, -1), preferred_element_typ...  16.6 us
    gather x8, local copies, waits for them, and re-layouts, shards(): jnp.take(returned, jnp.maximum(index, 0), axis=0).astype(jnp.float32)  13.8 us
    dot_general x1, matrix products, shards(): jnp.dot(rows, expert_in[0].reshape(half_width, -1), preferred_element_typ...  9.29 us
    all_to_all x1, starting transfers between devices, dispatch_rows(): lax.all_to_all(send_rows, ('dp', 'expert'), split_axis=0, concat_axis=0,...  6.91 us
  transfers between devices with their start and end apart: 8, of which 6 were waited for; matrix products, arithmetic and copies ran while one was open for 32% of the time, Pallas kernels for 0%

profile of v1, /device:TPU:8, one launch (start us, length us, event | category | flops | bytes accessed | tf_op | source)
XLA Modules:
  0.0 272.4 jit_solution(13596095282612889563)
XLA Ops:
  6.5 1.6 collective-permute-start
  9.6 16.4 %collective-permute-done = bf16[128,3072]{1,0:T(8,128)(2,1)S(1)} collective-permute-done((bf16[128,3072]{1,0:T(8,128)(2,1)}, bf16[128,3072]{1,0:T(8,128)(2,1)S(1)}, u32[]{:S(2)}, u32[]{:S(2)}) %collective-permute-start) | collective-permute-done | bytes 786464 | tf_op jit(solution)/shard_map/ppermute | solution.py:61
  26.0 1.6 collective-permute-start.1
  28.4 4.8 %select_reduce_fusion = (s32[128,8]{1,0:T(8,128)S(1)}, s32[128,8]{1,0:T(8,128)S(1)}) fusion(s32[384]{0:T(512)S(1)} %select_reduce_fusion.4, s32[128,8]{1,0:T(8,128)S(1)} %copy.22, s32[384]{0:T(512)S(1)} %select_reduce_fusion.5), kind=kLoop, calls=%fused_computation.16 | loop fusion | flops 1964032 | bytes 15360 | tf_op jit(solution)/shard_map/reduce_sum | solution.py:22
  35.2 10.3 %collective-permute-done.1 = bf16[128,3072]{1,0:T(8,128)(2,1)} collective-permute-done((bf16[128,3072]{1,0:T(8,128)(2,1)S(1)}, bf16[128,3072]{1,0:T(8,128)(2,1)}, u32[]{:S(2)}, u32[]{:S(2)}) %collective-permute-start.1) | collective-permute-done | bytes 786464 | tf_op jit(solution)/shard_map/ppermute | solution.py:61
  46.7 1.5 gather_fusion
  49.3 4.1 %copy.24 = bf16[384,8,2,256]{3,1,2,0:T(8,128)(2,1)} copy(bf16[384,8,2,256]{3,2,1,0:T(2,128)(2,1)} %bitcast.66) | data formatting | bytes 6291456
  53.5 4.6 %copy.21 = bf16[512,3072]{1,0:T(8,128)(2,1)} copy(bf16[512,3072]{0,1:T(8,128)(2,1)} %bitcast.65) | data formatting | bytes 6291456 | tf_op jit(solution)/shard_map/dot_general | solution.py:65
  58.1 7.3 %collective-permute-done.2 = bf16[128,3072]{1,0:T(8,128)(2,1)} collective-permute-done((bf16[128,3072]{1,0:T(8,128)(2,1)}, bf16[128,3072]{1,0:T(8,128)(2,1)}, u32[]{:S(2)}, u32[]{:S(2)}) %collective-permute-start.2) | collective-permute-done | bytes 786464 | tf_op jit(solution)/shard_map/ppermute | solution.py:61
  66.6 1.2 constant_dynamic-update-slice_fusion.6
  67.9 1.2 constant_dynamic-update-slice_fusion.3
  70.4 1.8 copy-done.3
  72.2 2.9 %fusion.5 = f32[512,2,256]{2,0,1:T(8,128)} fusion(bf16[2,256,3072]{2,1,0:T(8,128)(2,1)S(1)} %bitcast.67, bf16[1024,3072]{1,0:T(8,128)(2,1)S(1)} %constant_dynamic-update-slice_fusion, s32[]{:T(128)S(6)} %select_n.119), kind=kOutput, calls=%fused_computation.12 | convolution fusion | flops 1610612736 | bytes 7340036 | tf_op jit(solution)/shard_map/dot_general | solution.py:65
  76.2 6.9 %all-to-all-start = ((bf16[16,4,3072]{2,1,0:T(4,128)(2,1)}), bf16[16,4,3072]{2,1,0:T(4,128)(2,1)S(1)}, u32[]{:S(2)}, u32[]{:S(2)}) async-start(bf16[16,4,3072]{2,1,0:T(4,128)(2,1)} %select_select_fusion), calls=%async_computation.2 | async-start | bytes 786432 | tf_op jit(solution)/shard_map/all_to_all | solution.py:31
  83.4 13.0 %copy.25 = bf16[384,8,2,1024]{3,1,2,0:T(8,128)(2,1)} copy(bf16[384,8,2,1024]{3,2,1,0:T(2,128)(2,1)} %bitcast.64) | data formatting | bytes 25165824
  96.4 16.6 %copy.23 = bf16[2048,3072]{1,0:T(8,128)(2,1)} copy(bf16[2048,3072]{0,1:T(8,128)(2,1)} %bitcast.63) | data formatting | bytes 25165824 | tf_op jit(solution)/shard_map/dot_general | solution.py:71
  113.1 9.3 %fusion.21 = f32[64,2,1024]{2,0,1:T(8,128)} fusion(bf16[64,3072,1]{1,0,2:T(8,128)(2,1)S(1)} %reshape.214, bf16[2,1024,3072]{2,1,0:T(8,128)(2,1)} %bitcast.62), kind=kOutput, calls=%fused_computation.110 | convolution fusion | flops 805306368 | bytes 13500416 | tf_op jit(solution)/shard_map/dot_general | solution.py:71
  123.6 6.2 %all_gather.6 = bf16[512,256]{1,0:T(8,128)(2,1)S(1)} all-gather(bf16[512,128]{1,0:T(8,128)(2,1)S(1)} %fusion.10), channel_id=1, replica_groups=mesh['dp'=4,'expert'=4,'tensor'=2] {'tensor'}, dimensions={1}, use_global_device_ids=true | all-gather | bytes 393216 | tf_op jit(solution)/shard_map/all_gather | solution.py:80
  129.9 3.7 %fusion.20 = f32[512,3072]{1,0:T(8,128)} fusion(bf16[512,256]{1,0:T(8,128)(2,1)S(1)} %all_gather.6, bf16[256,3072]{1,0:T(8,128)(2,1)S(1)} %copy-done), kind=kOutput, calls=%fused_computation.109 | convolution fusion | flops 805306368 | bytes 8126464 | tf_op jit(solution)/shard_map/dot_general | solution.py:84
  135.4 2.4 reduce-scatter.8.cloned.1.call-done
  138.8 4.9 %all_gather.7 = bf16[64,1024]{1,0:T(8,128)(2,1)S(1)} all-gather(bf16[64,512]{1,0:T(8,128)(2,1)S(1)} %fusion.12), channel_id=1, replica_groups=mesh['dp'=4,'expert'=4,'tensor'=2] {'tensor'}, dimensions={1}, use_global_device_ids=true | all-gather | bytes 196608 | tf_op jit(solution)/shard_map/all_gather | solution.py:81
  143.7 4.1 %fusion.2 = bf16[64,3072]{1,0:T(8,128)(2,1)S(1)} fusion(bf16[64,1024]{1,0:T(8,128)(2,1)S(1)} %all_gather.7, bf16[1,1024,3072]{2,1,0:T(8,128)(2,1)} %param.15), kind=kOutput, calls=%fused_computation.11 | convolution fusion | flops 402849792 | bytes 6815744 | tf_op jit(solution)/shard_map/dot_general | solution.py:89
  148.8 6.0 %all-to-all-start.1 = ((bf16[16,4,3072]{2,1,0:T(4,128)(2,1)}), bf16[16,4,3072]{2,1,0:T(4,128)(2,1)S(1)}, u32[]{:S(2)}, u32[]{:S(2)}) async-start(bf16[16,4,3072]{2,1,0:T(4,128)(2,1)} %reshape.114), calls=%async_computation.4 | async-start | bytes 786432 | tf_op jit(solution)/shard_map/all_to_all | solution.py:35
  154.9 23.4 %all-to-all-done.1 = bf16[16,4,3072]{2,1,0:T(4,128)(2,1)S(1)} async-done(((bf16[16,4,3072]{2,1,0:T(4,128)(2,1)}), bf16[16,4,3072]{2,1,0:T(4,128)(2,1)S(1)}, u32[]{:S(2)}, u32[]{:S(2)}) %all-to-all-start.1) | async-done | bytes 393248 | tf_op jit(solution)/shard_map/all_to_all | solution.py:35
  180.4 1.9 gather_fusion.6
  182.3 2.0 gather_fusion.5
  184.3 2.0 gather_fusion.4
  186.3 1.9 gather_fusion.3
  188.2 2.0 gather_fusion.2
  190.2 1.9 gather_fusion.1
  192.1 67.2 %reduce-scatter.6.cloned.1.call-done = f32[128,3072]{1,0:T(8,128)} async-done(((f32[512,3072]{1,0:T(8,128)}), f32[128,3072]{1,0:T(8,128)}) %reduce-scatter.6.cloned.1.call-update) | async-done | bytes 1572880 | tf_op jit(solution)/shard_map/reduce_scatter | solution.py:83
  259.3 6.6 %add_convert_fusion = bf16[128,3072]{1,0:T(8,128)(2,1)} fusion(f32[128,3072]{1,0:T(8,128)} %reduce-scatter.6.cloned.1.call-done, bf16[128,3072]{1,0:T(8,128)(2,1)S(1)} %gather_fusion.8, bf16[128,3072]{1,0:T(8,128)(2,1)S(1)} %gather_fusion.7, bf16[128,3072]{1,0:T(8,128)(2,1)} %gather_fusion.6, bf16[128,3072]{1,0:T(8,128)(2,1)} %gather_fusion.5, ...), kind=kLoop, calls=%fused_computation.15 | loop fusion | flops 16121856 | bytes 8656896 | tf_op jit(solution)/shard_map/convert_element_type | solution.py:102
  (85 shorter events, 17.7 us)
Async XLA Ops:
  6.5 123.3 %copy-start = (bf16[256,3072]{1,0:T(8,128)(2,1)S(1)}, bf16[256,3072]{1,0:T(8,128)(2,1)}, u32[]{:S(2)}) copy-start(bf16[256,3072]{1,0:T(8,128)(2,1)} %param.17) | copy-start | bytes 4718596
  6.5 40.1 %copy-start.2 = (bf16[128,3072]{1,0:T(8,128)(2,1)S(1)}, bf16[128,3072]{1,0:T(8,128)(2,1)}, u32[]{:S(2)}) copy-start(bf16[128,3072]{1,0:T(8,128)(2,1)} %param.10) | copy-start | bytes 2359300
  6.5 116.0 %reduce-scatter.4.cloned.1.call-start = ((), (), s32[]{:S(2)}) async-start(), calls=%async_computation.5 | async-start | bytes 1572864 | tf_op jit(solution)/shard_map/reduce_scatter | solution.py:76
  6.5 19.5 %collective-permute-start = (bf16[128,3072]{1,0:T(8,128)(2,1)}, bf16[128,3072]{1,0:T(8,128)(2,1)S(1)}, u32[]{:S(2)}, u32[]{:S(2)}) collective-permute-start(bf16[128,3072]{1,0:T(8,128)(2,1)} %param.10), channel_id=1, source_target_pairs={{0,8},{8,16},{16,24},{24,0},{1,9},{9,17},{17,25},{25,1},{2,10},{10... | collective-permute-start | bytes 2359304 | tf_op jit(solution)/shard_map/ppermute | solution.py:61
  26.0 19.4 %collective-permute-start.1 = (bf16[128,3072]{1,0:T(8,128)(2,1)S(1)}, bf16[128,3072]{1,0:T(8,128)(2,1)}, u32[]{:S(2)}, u32[]{:S(2)}) collective-permute-start(bf16[128,3072]{1,0:T(8,128)(2,1)S(1)} %collective-permute-done), channel_id=1, source_target_pairs={{0,8},{8,16},{16,24},{24,0},{1,9},{9,17},{17,25},{25,1},{2,10},{10... | collective-permute-start | bytes 2359304 | tf_op jit(solution)/shard_map/ppermute | solution.py:61
  33.1 13.5 %copy-start.4 = (s32[128,8]{1,0:T(8,128)}, s32[128,8]{1,0:T(8,128)S(1)}, u32[]{:S(2)}) copy-start(s32[128,8]{1,0:T(8,128)S(1)} %get-tuple-element.22) | copy-start | bytes 12292
  33.1 13.5 %copy-start.6 = (s32[128,8]{1,0:T(8,128)}, s32[128,8]{1,0:T(8,128)S(1)}, u32[]{:S(2)}) copy-start(s32[128,8]{1,0:T(8,128)S(1)} %get-tuple-element.23) | copy-start | bytes 12292
  34.4 0.6 copy-start.8
  45.4 20.0 %collective-permute-start.2 = (bf16[128,3072]{1,0:T(8,128)(2,1)}, bf16[128,3072]{1,0:T(8,128)(2,1)}, u32[]{:S(2)}, u32[]{:S(2)}) collective-permute-start(bf16[128,3072]{1,0:T(8,128)(2,1)} %collective-permute-done.1), channel_id=1, source_target_pairs={{0,8},{8,16},{16,24},{24,0},{1,9},{9,17},{17,25},{25,1},{2,10},{10... | collective-permute-start | bytes 2359304 | tf_op jit(solution)/shard_map/ppermute | solution.py:61
  70.3 1.9 copy-start.3
  76.2 36.8 %all-to-all-start = ((bf16[16,4,3072]{2,1,0:T(4,128)(2,1)}), bf16[16,4,3072]{2,1,0:T(4,128)(2,1)S(1)}, u32[]{:S(2)}, u32[]{:S(2)}) async-start(bf16[16,4,3072]{2,1,0:T(4,128)(2,1)} %select_select_fusion), calls=%async_computation.2 | async-start | bytes 786432 | tf_op jit(solution)/shard_map/all_to_all | solution.py:31
  83.1 54.6 %reduce-scatter.8.cloned.1.call-start = ((), (), s32[]{:S(2)}) async-start(), calls=%async_computation.7 | async-start | bytes 786432 | tf_op jit(solution)/shard_map/reduce_scatter | solution.py:77
  122.4 136.9 %reduce-scatter.6.cloned.1.call-start = ((), (), s32[]{:S(2)}) async-start(), calls=%async_computation.6 | async-start | bytes 7864320 | tf_op jit(solution)/shard_map/reduce_scatter | solution.py:83
  133.5 0.8 copy-start.5
  133.5 0.9 copy-start.7
  133.5 0.9 copy-start.9
  147.8 7.0 %copy-start.10 = (s32[128,8]{0,1:T(8,128)S(1)}, s32[128,8]{0,1:T(8,128)}, u32[]{:S(2)}) copy-start(s32[128,8]{0,1:T(8,128)} %param.12) | copy-start | bytes 12292
  148.8 29.5 %all-to-all-start.1 = ((bf16[16,4,3072]{2,1,0:T(4,128)(2,1)}), bf16[16,4,3072]{2,1,0:T(4,128)(2,1)S(1)}, u32[]{:S(2)}, u32[]{:S(2)}) async-start(bf16[16,4,3072]{2,1,0:T(4,128)(2,1)} %reshape.114), calls=%async_computation.4 | async-start | bytes 786432 | tf_op jit(solution)/shard_map/all_to_all | solution.py:35
  259.3 6.6 %copy-start.1 = (bf16[256,3072]{1,0:T(8,128)(2,1)S(1)}, bf16[256,3072]{1,0:T(8,128)(2,1)}, u32[]{:S(2)}) copy-start(bf16[256,3072]{1,0:T(8,128)(2,1)} %param.17) | copy-start | bytes 4718596
Sparse Core Ops, SparseCore 0:
  75.2 21.2 reduce-scatter.3
  122.6 15.1 reduce-scatter.7
  140.1 119.1 reduce-scatter.5
